TPU v7x, 512 devices: a whole 4x8x8 slice. The times are simulated.
512 devices in a mesh: rows: 512 (over z, y, x, core).
Axes of the slice: x: 4, y: 8, z: 8, core: 2. Of those that a mesh axis runs over, the one named last changes fastest.
Arguments:
- adj_diag: int32 [8192, 512], P('rows'), may hold values from -2147483648 to 2147483647
- adj_right: int32 [8192, 512], P('rows'), may hold values from -2147483648 to 2147483647
- alive_diag: int32 [8192, 512], P('rows'), may hold values from -2147483648 to 2147483647
- alive_right: int32 [8192, 512], P('rows'), may hold values from -2147483648 to 2147483647
- truss_k: int32 [1], replicated, may hold values from 130 to 193
Outputs:
- support_field: float32 [262144, 1024], P('rows')
- removed_counts: int32 [3], replicated
All inputs are finite; a program needn't handle non-finite values.
Results may differ from a plain program's by a relative error of at most 0.0003.
Values may be sent and summed in bfloat16 or wider, within the bound.
A program may use at most 64 MiB of HBM per device.

v0:
```python
import functools

import jax
import jax.numpy as jnp
from jax import lax
from jax.experimental import pallas as pl
from jax.experimental.pallas import tpu as pltpu
from jax.sharding import PartitionSpec as P

F8 = jnp.float8_e4m3fn
F32 = jnp.float32
WORD = 32
ITERS = 3


def dot_nt(lhs, rhs):
    return lax.dot_general(lhs, rhs, (((1,), (1,)), ((), ())), preferred_element_type=F32)


def send(src, dst, send_sem, recv_sem, target):
    return pltpu.make_async_remote_copy(
        src_ref=src,
        dst_ref=dst,
        send_sem=send_sem,
        recv_sem=recv_sem,
        device_id=(target,),
        device_id_type=pl.DeviceIdType.MESH,
    )


def kernel(
    n, k_ref, ad_ref, ar_ref, ld_ref, lr_ref, out_ref, cnt_ref,
    k_smem, raw, own, halo, x, eye, tri, spare, psum_in, psum_next, psum_btw, mine, gathered,
    k_sem, raw_sems, send_sems, recv_sems, relay_sems, cnt_send, cnt_recv,
):
    t = ad_ref.shape[1]
    words = ad_ref.shape[0]
    me = lax.axis_index("rows")
    even = lax.rem(me, 2) == 0
    barrier = pltpu.get_barrier_semaphore()

    def greet(d, carry):
        pl.semaphore_signal(
            barrier, inc=1, device_id=(lax.rem(me + d, n),), device_id_type=pl.DeviceIdType.MESH
        )
        return carry

    lax.fori_loop(1, n, greet, 0)
    loads = [
        pltpu.make_async_copy(src, raw.at[i], raw_sems.at[i])
        for i, src in enumerate((ad_ref, ar_ref, ld_ref, lr_ref))
    ]
    for load in loads:
        load.start()
    k_load = pltpu.make_async_copy(k_ref, k_smem, k_sem)
    k_load.start()
    for load in loads:
        load.wait()
    own[0] = raw[0] & raw[2]
    own[1] = raw[1] & raw[3]

    AT, W, A = (pl.ds(i * t, t) for i in range(3))
    shift = lax.broadcasted_iota(jnp.int32, (WORD, t), 0)
    col = lax.broadcasted_iota(jnp.int32, (WORD, t), 1)

    half = t // 2

    def unpack(src, upper):
        for w in range(words):
            left = half if upper and 2 * w >= words else 0
            bits = (jnp.broadcast_to(src[w : w + 1, left:], (WORD, t - left)) >> shift[:, left:]) & 1
            if upper:
                bits = jnp.where(col[:, left:] - shift[:, left:] > WORD * w, bits, 0)
            yield pl.ds(WORD * w, WORD), pl.ds(left, t - left), bits.astype(F32).astype(F8)

    def put_across(src, j):
        for rows, _, bits in unpack(src, False):
            x[j, rows, A] = bits

    def put_transposed(j):
        x[j + 1, :, AT] = dot_nt(eye[...], x[j, :, A]).astype(F8)

    def put_within(src, j):
        for rows, cols, bits in unpack(src, True):
            tri[rows, cols] = bits
        flipped = dot_nt(eye[...], tri[...])
        x[j, :, W] = (flipped + tri[...].astype(F32)).astype(F8)

    row_id = lax.broadcasted_iota(jnp.int32, (t, t), 0)
    col_id = lax.broadcasted_iota(jnp.int32, (t, t), 1)
    eye[...] = jnp.where(row_id == col_id, 1.0, 0.0).astype(F32).astype(F8)
    tri[half:, :half] = jnp.zeros((t - half, half), F32).astype(F8)

    pl.semaphore_wait(barrier, n - 1)
    top, low = pl.ds(0, words // 2), pl.ds(words // 2, words // 2)
    whole, right = pl.ds(0, t), pl.ds(half, half)

    def pieces(source, slot, by, sends):
        parts = [(top, whole), (low, right if slot in (1, 3, 5) else whole)]
        return [
            send(
                source.at[rows, cols], halo.at[slot, rows, cols],
                sends.at[i], recv_sems.at[2 * slot + i], lax.rem(me + by + n, n),
            )
            for i, (rows, cols) in enumerate(parts)
        ]

    def start(slot):
        for piece in copies[slot]:
            piece.start()

    def arrive(slot):
        for piece in copies[slot]:
            piece.wait_recv()

    def left(copy):
        for piece in copy:
            piece.wait_send()

    routes = {2: (1, 1), 3: (0, -1), 1: (0, 1), 4: (1, -1), 0: (1, 2), 5: (0, -2)}
    copies = {
        slot: pieces(own.at[what], slot, by, send_sems.at[slot])
        for slot, (what, by) in routes.items()
    }
    to_right = pieces(halo.at[2], 0, 1, relay_sems)
    to_left = pieces(halo.at[3], 5, -1, relay_sems)
    start(3)
    start(2)

    @pl.when(even)
    def _():
        start(0)

    @pl.when(jnp.logical_not(even))
    def _():
        start(5)

    start(4)
    start(1)
    put_across(own.at[1], 1)

    k_load.wait()
    thresh = (k_smem[0] - 2).astype(F32)

    put_within(own.at[0], 1)
    put_transposed(1)
    psum_in[...] = dot_nt(x[1, :, t:], x[1, :, t:])
    psum_next[...] = dot_nt(x[2, :, AT], x[2, :, AT])
    psum_btw[...] = dot_nt(x[1, :, W], x[2, :, AT])

    def total(values):
        lanes = jnp.sum(values, axis=0, keepdims=True)
        return sum(lanes[:, i : i + 128] for i in range(0, t, 128))

    def keep(support, j, part):
        old = x[j, :, part].astype(F32)
        return old, jnp.where(support >= thresh, old, 0.0)

    def inside(j):
        return dot_nt(x[j], x[j])

    def between(j):
        return dot_nt(x[j, :, t:], x[j + 1, :, : 2 * t])

    counts = []

    def own_count(old_w, new_w, old_a, new_a):
        counts.append(total((old_w - new_w) + 2.0 * (old_a - new_a)))

    arrive(2)

    @pl.when(even)
    def _():
        for piece in to_right:
            piece.start()

    put_across(halo.at[2], 0)
    put_transposed(0)
    old_w, w0 = keep(psum_in[...] + dot_nt(x[1, :, AT], x[1, :, AT]), 1, W)
    arrive(1)
    put_within(halo.at[1], 0)
    _, am = keep(between(0), 0, A)
    arrive(3)

    @pl.when(jnp.logical_not(even))
    def _():
        for piece in to_left:
            piece.start()

    arrive(0)
    for rows, _, bits in unpack(halo.at[0], False):
        spare[rows, :] = bits
    x[0, :, AT] = dot_nt(eye[...], spare[...]).astype(F8)
    _, wm = keep(inside(0), 0, W)
    put_within(halo.at[3], 2)
    old_a, a0 = keep(psum_btw[...] + dot_nt(x[1, :, A], x[2, :, W]), 1, A)
    own_count(old_w, w0, old_a, a0)
    arrive(4)
    put_across(halo.at[4], 2)
    put_transposed(2)
    _, w1 = keep(psum_next[...] + dot_nt(x[2, :, t:], x[2, :, t:]), 2, W)
    arrive(5)
    put_within(halo.at[5], 3)
    _, a1 = keep(between(2), 2, A)
    x[0, :, W] = wm.astype(F8)
    x[0, :, A] = am.astype(F8)
    x[1, :, W] = w0.astype(F8)
    x[1, :, A] = a0.astype(F8)
    x[2, :, W] = w1.astype(F8)
    x[2, :, A] = a1.astype(F8)
    put_transposed(0)
    put_transposed(1)

    _, am = keep(between(0), 0, A)
    old_w, w0 = keep(inside(1), 1, W)
    old_a, a0 = keep(between(1), 1, A)
    own_count(old_w, w0, old_a, a0)
    _, w1 = keep(inside(2), 2, W)
    x[0, :, A] = am.astype(F8)
    x[1, :, W] = w0.astype(F8)
    x[1, :, A] = a0.astype(F8)
    x[2, :, W] = w1.astype(F8)
    put_transposed(0)
    put_transposed(1)

    support_w = inside(1)
    old_w, w0 = keep(support_w, 1, W)
    support_a = between(1)
    old_a, a0 = keep(support_a, 1, A)
    own_count(old_w, w0, old_a, a0)
    lane = lax.broadcasted_iota(jnp.int32, (1, 128), 1)
    packed = jnp.zeros((1, 128), F32)
    for step, row in enumerate(counts):
        packed = jnp.where(lane == step, jnp.sum(row, axis=1, keepdims=True), packed)
    mine[...] = packed.astype(jnp.int32)

    def share(d, carry):
        send(mine, gathered.at[d - 1], cnt_send, cnt_recv, lax.rem(me + d, n)).start()
        return carry

    lax.fori_loop(1, n, share, 0)
    out_ref[:, :t] = support_w * w0
    out_ref[:, t:] = support_a * a0
    for slot in range(1, 5):
        left(copies[slot])

    @pl.when(even)
    def _():
        left(copies[0])
        left(to_right)

    @pl.when(jnp.logical_not(even))
    def _():
        left(copies[5])
        left(to_left)

    pltpu.make_async_copy(gathered, gathered, cnt_recv).wait()
    cnt_ref[: n - 1] = gathered[...]
    cnt_ref[n - 1] = mine[...]
    pltpu.make_async_copy(gathered, gathered, cnt_send).wait()


def finish(support_ref, cnt_ref, out_ref, removed_ref, sems):
    parts = sems.shape[0]
    rows = support_ref.shape[0] // parts
    copies = [
        pltpu.make_async_copy(
            support_ref.at[pl.ds(i * rows, rows)], out_ref.at[pl.ds(i * rows, rows)], sems.at[i]
        )
        for i in range(parts)
    ]
    for copy in copies:
        copy.start()
    summed = jnp.sum(cnt_ref[...], axis=0)
    lane = lax.broadcasted_iota(jnp.int32, summed.shape, 1)
    for step in range(removed_ref.shape[0]):
        removed_ref[step] = jnp.sum(jnp.where(lane == step, summed, 0)) // 2
    for copy in copies:
        copy.wait()


def on_device(n, adj_diag, adj_right, alive_diag, alive_right, truss_k):
    words, t = adj_diag.shape
    vmem = pl.BlockSpec(memory_space=pltpu.VMEM)
    smem = pl.BlockSpec(memory_space=pltpu.SMEM)
    hbm = pl.BlockSpec(memory_space=pltpu.HBM)
    args = [
        pltpu.with_memory_space_constraint(v, pltpu.HBM)
        for v in (adj_diag, adj_right, alive_diag, alive_right)
    ]
    support, counts = pl.pallas_call(
        functools.partial(kernel, n),
        out_shape=(
            jax.ShapeDtypeStruct((t, 2 * t), F32),
            jax.ShapeDtypeStruct((n, 1, 128), jnp.int32),
        ),
        in_specs=[hbm] * 5,
        out_specs=(vmem, vmem),
        scratch_shapes=[
            pltpu.SMEM((1,), jnp.int32),
            pltpu.VMEM((4, words, t), jnp.int32),
            pltpu.VMEM((2, words, t), jnp.int32),
            pltpu.VMEM((6, words, t), jnp.int32),
            pltpu.VMEM((4, t, 3 * t), F8),
            pltpu.VMEM((t, t), F8),
            pltpu.VMEM((t, t), F8),
            pltpu.VMEM((t, t), F8),
            pltpu.VMEM((t, t), F32),
            pltpu.VMEM((t, t), F32),
            pltpu.VMEM((t, t), F32),
            pltpu.VMEM((1, 128), jnp.int32),
            pltpu.VMEM((n - 1, 1, 128), jnp.int32),
            pltpu.SemaphoreType.DMA,
            pltpu.SemaphoreType.DMA((4,)),
            pltpu.SemaphoreType.DMA((6, 2)),
            pltpu.SemaphoreType.DMA((12,)),
            pltpu.SemaphoreType.DMA((2,)),
            pltpu.SemaphoreType.DMA,
            pltpu.SemaphoreType.DMA,
        ],
        compiler_params=pltpu.CompilerParams(collective_id=0, has_side_effects=True, vmem_limit_bytes=24 * 2**20),
    )(truss_k, *args)
    return pl.pallas_call(
        finish,
        out_shape=(
            jax.ShapeDtypeStruct((t, 2 * t), F32),
            jax.ShapeDtypeStruct((ITERS,), jnp.int32),
        ),
        in_specs=[vmem, vmem],
        out_specs=(hbm, smem),
        scratch_shapes=[pltpu.SemaphoreType.DMA((4,))],
        compiler_params=pltpu.CompilerParams(vmem_limit_bytes=2**20),
    )(support, counts)


def solution(mesh):
    row = P("rows", None)
    return jax.shard_map(
        functools.partial(on_device, mesh.shape["rows"]),
        mesh=mesh,
        in_specs=(row, row, row, row, P()),
        out_specs=(row, P()),
        check_vma=False,
    )
```

profile of v0, /device:TPU:1, one launch (start us, length us, event | category | flops | bytes accessed | tf_op | source)
XLA Modules:
  0.0 48.7 jit_solution(2566122694927808215)
XLA Ops:
  1.3 45.5 %shard_map.68 = (f32[512,1024]{1,0:T(8,128)S(1)}, s32[512,1,128]{2,1,0:T(1,128)S(1)}) custom-call(s32[1]{0:T(128)S(6)} %copy.7.k_ref, s32[16,512]{1,0:T(8,128)} %ad_ref.1, s32[16,512]{1,0:T(8,128)} %ar_ref.1, s32[16,512]{1,0:T(8,128)} %ld_ref.1, s32[16,512]{1,0:T(8,128)} %lr_ref.1), custom_call_target="tpu_custom_call" | custom-call | tf_op jit(solution)/shard_map/pallas_call | solution.py:291
  46.7 2.0 %shard_map.69 = (f32[512,1024]{1,0:T(8,128)}, s32[3]{0:T(128)}) custom-call(f32[512,1024]{1,0:T(8,128)S(1)} %get-tuple-element.4.support_ref, s32[512,1,128]{2,1,0:T(1,128)S(1)} %get-tuple-element.5.cnt_ref), custom_call_target="tpu_custom_call" | custom-call | tf_op jit(solution)/shard_map/pallas_call | solution.py:323
where the time goes:
time: 48.9 us; the launch traced here: 48.7 us
  Pallas kernels  47.5 us (97%)
  between operations  1.29 us (3%)
    pallas_call x1, Pallas kernels, on_device(): pl.pallas_call(functools.partial(kernel, n), out_shape=(jax.ShapeDtypeStr...  45.5 us
    pallas_call x1, Pallas kernels, on_device(): pl.pallas_call(finish, out_shape=(jax.ShapeDtypeStruct((t, 2 * t), F32),...  2 us

commit v1 on v0

v1 whole, which is shorter than its diff:
```python
import functools

import jax
import jax.numpy as jnp
from jax import lax
from jax.experimental import pallas as pl
from jax.experimental.pallas import tpu as pltpu
from jax.sharding import PartitionSpec as P

F8 = jnp.float8_e4m3fn
F32 = jnp.float32
WORD = 32
ITERS = 3
ROW = 16


def dot_nt(lhs, rhs):
    return lax.dot_general(lhs, rhs, (((1,), (1,)), ((), ())), preferred_element_type=F32)


def dot_nn(lhs, rhs):
    return lax.dot_general(lhs, rhs, (((1,), (0,)), ((), ())), preferred_element_type=F32)


def send(src, dst, send_sem, recv_sem, target):
    return pltpu.make_async_remote_copy(
        src_ref=src,
        dst_ref=dst,
        send_sem=send_sem,
        recv_sem=recv_sem,
        device_id=(target,),
        device_id_type=pl.DeviceIdType.MESH,
    )


def greet(barrier, target):
    pl.semaphore_signal(
        barrier, inc=1, device_id=(target,), device_id_type=pl.DeviceIdType.MESH
    )


def set_eye(eye):
    half = eye.shape[0]
    row_id = lax.broadcasted_iota(jnp.int32, (half, half), 0)
    col_id = lax.broadcasted_iota(jnp.int32, (half, half), 1)
    eye[...] = jnp.where(row_id == col_id, 1.0, 0.0).astype(F32).astype(F8)


def turned(eye, block):
    return dot_nt(eye[...], block)


def transpose(eye, src, dst):
    half = eye.shape[0]
    lo, hi = pl.ds(0, half), pl.ds(half, half)
    for i in (lo, hi):
        for j in (lo, hi):
            dst[i, j] = turned(eye, src[j, i]).astype(F8)


def bits_of(row, shift):
    return (jnp.broadcast_to(row, (WORD, row.shape[1])) >> shift[:, : row.shape[1]]) & 1


def as_f8(bits):
    return bits.astype(F32).astype(F8)


def unpack_across(src, *dsts):
    words, t = src.shape
    shift = lax.broadcasted_iota(jnp.int32, (WORD, t), 0)
    for w in range(words):
        bits = as_f8(bits_of(src[w : w + 1, :], shift))
        for dst in dsts:
            dst[pl.ds(WORD * w, WORD), :] = bits


def unpack_within(src, eye, tri, *dsts):
    words, t = src.shape
    half = t // 2
    shift = lax.broadcasted_iota(jnp.int32, (WORD, half), 0)
    ahead = lax.broadcasted_iota(jnp.int32, (WORD, half), 1) - shift
    lo, hi = pl.ds(0, half), pl.ds(half, half)
    for w in range(words):
        rows = pl.ds(WORD * w, WORD)
        top = 2 * w < words
        part = slice(0, half) if top else slice(half, t)
        bits = bits_of(src[w : w + 1, part], shift)
        first = WORD * w if top else WORD * w - half
        tri[rows, :] = as_f8(jnp.where(ahead > first, bits, 0))
        if top:
            bits = as_f8(bits_of(src[w : w + 1, half:], shift))
            for dst in dsts:
                dst[rows, hi] = bits
    for i in (lo, hi):
        both = (turned(eye, tri[i, :]) + tri[i, :].astype(F32)).astype(F8)
        for dst in dsts:
            dst[i, i] = both
    corner = turned(eye, dsts[0][lo, hi]).astype(F8)
    for dst in dsts:
        dst[hi, lo] = corner


def keep(support, thresh, old):
    old = old.astype(F32)
    return old, jnp.where(support >= thresh, old, 0.0)


def total(values):
    t = values.shape[0]
    lanes = jnp.sum(values, axis=0, keepdims=True)
    return sum(lanes[:, i : i + 128] for i in range(0, t, 128))


def removed(old_w, new_w, old_a, new_a):
    return total((old_w - new_w) + 2.0 * (old_a - new_a))


def first(
    n, k_ref, ad_ref, ar_ref, ld_ref, lr_ref,
    late, hm_out, w1_out, am_out, w0_out, a0_out, next_out, cnt_out,
    k_smem, raw, own, halo, h1, v, vm, at, atm, eye, tri, psum_in, psum_btw,
    k_sem, raw_sems, send_sems, recv_sems,
):
    words, t = ad_ref.shape
    half = t // 2
    me = lax.axis_index("rows")
    barrier = pltpu.get_barrier_semaphore()
    near = {by: lax.rem(me + by + n, n) for by in (1, -1, 2, -2)}
    for target in near.values():
        greet(barrier, target)
    loads = [
        pltpu.make_async_copy(src, raw.at[i], raw_sems.at[i])
        for i, src in enumerate((ad_ref, ar_ref, ld_ref, lr_ref))
    ]
    for load in loads:
        load.start()
    k_load = pltpu.make_async_copy(k_ref, k_smem, k_sem)
    k_load.start()
    for load in loads:
        load.wait()
    own[0] = raw[0] & raw[2]
    own[1] = raw[1] & raw[3]
    set_eye(eye)
    pl.semaphore_wait(barrier, 4)

    low = words // 2
    copies = {}
    sem = 0
    for slot, what, by in ((3, 0, -1), (2, 1, 1), (1, 0, 1), (5, 0, -2), (0, 1, 2), (4, 1, -1)):
        if what:
            parts = [(pl.ds(0, words), pl.ds(0, t))]
        else:
            parts = [(pl.ds(0, low), pl.ds(0, t)), (pl.ds(low, words - low), pl.ds(half, half))]
        copies[slot] = []
        for rows, cols in parts:
            copies[slot].append(send(
                own.at[what, rows, cols], halo.at[slot, rows, cols],
                send_sems.at[sem], recv_sems.at[sem], near[by],
            ))
            sem += 1
        for piece in copies[slot]:
            piece.start()

    def arrive(slot):
        for piece in copies[slot]:
            piece.wait_recv()

    W, A = pl.ds(0, t), pl.ds(t, t)
    unpack_across(own.at[1], h1.at[:, A], v.at[W, :])
    unpack_within(own.at[0], eye, tri, h1.at[:, W], vm.at[A, :])
    transpose(eye, v.at[W, :], at)
    psum_in[...] = dot_nt(h1[...], h1[...])
    next_out[...] = dot_nt(at[...], at[...])
    psum_btw[...] = dot_nn(h1[:, W], v[W, :])
    k_load.wait()
    thresh = (k_smem[0] - 2).astype(F32)

    arrive(2)
    unpack_across(halo.at[2], hm_out.at[:, A], vm.at[W, :])
    transpose(eye, vm.at[W, :], atm)
    old_w, new_w = keep(psum_in[...] + dot_nt(atm[...], atm[...]), thresh, h1[:, W])
    w0_out[...] = new_w.astype(F8)
    arrive(1)
    unpack_within(halo.at[1], eye, tri, hm_out.at[:, W])
    _, new = keep(dot_nn(hm_out[...], vm[...]), thresh, hm_out[:, A])
    am_out[...] = new.astype(F8)
    arrive(3)
    unpack_within(halo.at[3], eye, tri, w1_out, v.at[A, :])
    old_a, new_a = keep(psum_btw[...] + dot_nn(h1[:, A], v[A, :]), thresh, h1[:, A])
    a0_out[...] = new_a.astype(F8)
    cnt_out[...] = removed(old_w, new_w, old_a, new_a)
    for i, slot in enumerate((0, 4, 5)):
        arrive(slot)
        late[i] = halo[slot]
    for pieces in copies.values():
        for piece in pieces:
            piece.wait_send()


def second(
    n, k_ref, late, hm, w1, am, w0, a0, psum_next, cnt1,
    out_ref, cnt_ref,
    k_smem, spare, atm, h2, v2, g0, u0, g1, u1, g2, at0, at1, r1, q1, at2, eye, tri,
    mine, mine2, row_in, col_in,
    k_sem, row_send, row_recv, col_send, col_recv,
):
    t = w1.shape[0]
    me = lax.axis_index("rows")
    rows = n // ROW
    place, line = lax.rem(me, ROW), lax.div(me, ROW)
    barrier = pltpu.get_barrier_semaphore()

    def beside(d):
        return line * ROW + lax.rem(place + d, ROW)

    def across(d):
        return lax.rem(line + d, rows) * ROW + place

    def greet_row(d, carry):
        greet(barrier, beside(d))
        return carry

    def greet_col(d, carry):
        greet(barrier, across(d))
        return carry

    lax.fori_loop(1, rows, greet_col, 0)
    lax.fori_loop(1, ROW, greet_row, 0)
    k_load = pltpu.make_async_copy(k_ref, k_smem, k_sem)
    k_load.start()
    set_eye(eye)
    W, A = pl.ds(0, t), pl.ds(t, t)

    unpack_across(late.at[0], spare)
    transpose(eye, spare, atm)
    h2[:, W] = w1[...]
    unpack_across(late.at[1], h2.at[:, A], v2.at[W, :])
    unpack_within(late.at[2], eye, tri, v2.at[A, :])
    k_load.wait()
    thresh = (k_smem[0] - 2).astype(F32)

    _, new = keep(dot_nt(hm[...], hm[...]) + dot_nt(atm[...], atm[...]), thresh, hm[:, W])
    g0[:, W] = new.astype(F8)
    g0[:, A] = am[...]
    u0[W, :] = am[...]
    u0[A, :] = w0[...]
    g1[:, W] = w0[...]
    g1[:, A] = a0[...]
    u1[W, :] = a0[...]
    transpose(eye, am, at0)
    transpose(eye, a0, at1)
    _, new = keep(psum_next[...] + dot_nt(h2[...], h2[...]), thresh, w1[...])
    u1[A, :] = new.astype(F8)
    g2[:, W] = new.astype(F8)
    _, new = keep(dot_nn(h2[...], v2[...]), thresh, h2[:, A])
    g2[:, A] = new.astype(F8)

    _, new = keep(dot_nn(g0[...], u0[...]), thresh, g0[:, A])
    spare[...] = new.astype(F8)
    old_w, new_w = keep(dot_nt(at0[...], at0[...]) + dot_nt(g1[...], g1[...]), thresh, g1[:, W])
    r1[:, W] = new_w.astype(F8)
    old_a, new_a = keep(dot_nn(g1[...], u1[...]), thresh, g1[:, A])
    r1[:, A] = new_a.astype(F8)
    q1[W, :] = new_a.astype(F8)
    cnt2 = removed(old_w, new_w, old_a, new_a)
    transpose(eye, spare, at2)
    _, new = keep(dot_nt(at1[...], at1[...]) + dot_nt(g2[...], g2[...]), thresh, g2[:, W])
    q1[A, :] = new.astype(F8)

    support_w = dot_nt(at2[...], at2[...]) + dot_nt(r1[...], r1[...])
    old_w, new_w = keep(support_w, thresh, r1[:, W])
    out_ref[:, W] = support_w * new_w
    support_a = dot_nn(r1[...], q1[...])
    old_a, new_a = keep(support_a, thresh, r1[:, A])
    out_ref[:, A] = support_a * new_a
    lane = lax.broadcasted_iota(jnp.int32, (1, 128), 1)
    packed = jnp.zeros((1, 128), F32)
    for step, row in enumerate((cnt1[...], cnt2, removed(old_w, new_w, old_a, new_a))):
        packed = jnp.where(lane == step, jnp.sum(row, axis=1, keepdims=True), packed)
    mine[...] = packed.astype(jnp.int32)
    pl.semaphore_wait(barrier, rows + ROW - 2)

    def share_row(d, carry):
        send(mine, row_in.at[d - 1], row_send, row_recv, beside(d)).start()
        return carry

    def share_col(d, carry):
        send(mine2, col_in.at[d - 1], col_send, col_recv, across(d)).start()
        return carry

    lax.fori_loop(1, ROW, share_row, 0)
    pltpu.make_async_copy(row_in, row_in, row_recv).wait()
    mine2[...] = mine[...] + jnp.sum(row_in[...], axis=0)
    lax.fori_loop(1, rows, share_col, 0)
    pltpu.make_async_copy(row_in, row_in, row_send).wait()
    pltpu.make_async_copy(col_in, col_in, col_recv).wait()
    cnt_ref[...] = mine2[...] + jnp.sum(col_in[...], axis=0)
    pltpu.make_async_copy(col_in, col_in, col_send).wait()


def finish(support_ref, cnt_ref, out_ref, removed_ref, sums, sems, sum_sem):
    parts = sems.shape[0]
    rows = support_ref.shape[0] // parts
    copies = [
        pltpu.make_async_copy(
            support_ref.at[pl.ds(i * rows, rows)], out_ref.at[pl.ds(i * rows, rows)], sems.at[i]
        )
        for i in range(parts)
    ]
    for copy in copies:
        copy.start()
    lane = lax.broadcasted_iota(jnp.int32, cnt_ref.shape, 1)
    for step in range(ITERS):
        sums[step] = jnp.sum(jnp.where(lane == step, cnt_ref[...], 0)) // 2
    last = pltpu.make_async_copy(sums, removed_ref, sum_sem)
    last.start()
    for copy in copies:
        copy.wait()
    last.wait()


def on_device(n, adj_diag, adj_right, alive_diag, alive_right, truss_k):
    words, t = adj_diag.shape
    half = t // 2
    vmem = pl.BlockSpec(memory_space=pltpu.VMEM)
    hbm = pl.BlockSpec(memory_space=pltpu.HBM)
    args = [
        pltpu.with_memory_space_constraint(v, pltpu.HBM)
        for v in (adj_diag, adj_right, alive_diag, alive_right)
    ]
    dma = pltpu.SemaphoreType.DMA
    tile, wide, tall = (pltpu.VMEM(s, F8) for s in ((t, t), (t, 2 * t), (2 * t, t)))
    f32 = pltpu.VMEM((t, t), F32)
    row = pltpu.VMEM((1, 128), jnp.int32)
    eye, tri = pltpu.VMEM((half, half), F8), pltpu.VMEM((t, half), F8)
    shape = jax.ShapeDtypeStruct
    parts = pl.pallas_call(
        functools.partial(first, n),
        out_shape=(
            shape((3, words, t), jnp.int32),
            shape((t, 2 * t), F8),
            shape((t, t), F8),
            shape((t, t), F8),
            shape((t, t), F8),
            shape((t, t), F8),
            shape((t, t), F32),
            shape((1, 128), F32),
        ),
        in_specs=[hbm] * 5,
        out_specs=(vmem,) * 8,
        scratch_shapes=[
            pltpu.SMEM((1,), jnp.int32),
            pltpu.VMEM((4, words, t), jnp.int32),
            pltpu.VMEM((2, words, t), jnp.int32),
            pltpu.VMEM((6, words, t), jnp.int32),
            wide, tall, tall, tile, tile, eye, tri, f32, f32,
            dma, dma((4,)), dma((9,)), dma((9,)),
        ],
        compiler_params=pltpu.CompilerParams(collective_id=0, has_side_effects=True, vmem_limit_bytes=24 * 2**20),
    )(truss_k, *args)
    support, counts = pl.pallas_call(
        functools.partial(second, n),
        out_shape=(shape((t, 2 * t), F32), shape((1, 128), jnp.int32)),
        in_specs=[hbm] + [vmem] * 8,
        out_specs=(vmem, vmem),
        scratch_shapes=[
            pltpu.SMEM((1,), jnp.int32),
            tile, tile, wide, tall, wide, tall, wide, tall, wide, tile, tile, wide, tall, tile, eye, tri,
            row, row,
            pltpu.VMEM((ROW - 1, 1, 128), jnp.int32),
            pltpu.VMEM((n // ROW - 1, 1, 128), jnp.int32),
            dma, dma, dma, dma, dma,
        ],
        compiler_params=pltpu.CompilerParams(collective_id=1, has_side_effects=True, vmem_limit_bytes=24 * 2**20),
    )(truss_k, *parts)
    return pl.pallas_call(
        finish,
        out_shape=(shape((t, 2 * t), F32), shape((ITERS,), jnp.int32)),
        in_specs=[vmem, vmem],
        out_specs=(hbm, hbm),
        scratch_shapes=[pltpu.SMEM((ITERS,), jnp.int32), dma((16,)), dma],
        compiler_params=pltpu.CompilerParams(vmem_limit_bytes=2**20),
    )(support, counts)


def solution(mesh):
    row = P("rows", None)
    return jax.shard_map(
        functools.partial(on_device, mesh.shape["rows"]),
        mesh=mesh,
        in_specs=(row, row, row, row, P()),
        out_specs=(row, P()),
        check_vma=False,
    )
```

time: 48.9 us -> 38.3 us (0.78)
  Pallas kernels: 47.5 us -> 36.8 us
    pallas_call x2 -> x3, Pallas kernels: 47.5 us -> 36.8 us  [the longest x1 19.1 us: on_device(): pl.pallas_call(functools.partial(first, n), out_shape=(shape((3, words, t...]
where the time goes in v1:
time: 38.3 us; the launch traced here: 38.1 us
  Pallas kernels  36.8 us (96%)
  between operations  1.29 us (3%)
    pallas_call x1, Pallas kernels, on_device(): pl.pallas_call(functools.partial(first, n), out_shape=(shape((3, words, t...  19.1 us
    pallas_call x1, Pallas kernels, on_device(): pl.pallas_call(functools.partial(second, n), out_shape=(shape((t, 2 * t),...  16.2 us
    pallas_call x1, Pallas kernels, on_device(): pl.pallas_call(finish, out_shape=(shape((t, 2 * t), F32), shape((ITERS,),...  1.46 us

profile of v1, /device:TPU:1, one launch (start us, length us, event | category | flops | bytes accessed | tf_op | source)
XLA Modules:
  0.0 38.1 jit_solution(7212064438998922084)
XLA Ops:
  1.3 19.1 %shard_map.68 = (s32[3,16,512]{2,1,0:T(8,128)S(1)}, f8e4m3fn[512,1024]{1,0:T(32,128)(4,1)S(1)}, f8e4m3fn[512,512]{1,0:T(32,128)(4,1)S(1)}, f8e4m3fn[512,512]{1,0...) custom-call(s32[1]{0:T(128)S(6)} %copy.7.k_ref, ...), custom_call_target="tpu_custom_call" | custom-call | tf_op jit(solution)/shard_map/pallas_call | solution.py:338
  20.4 16.2 %shard_map.69 = (f32[512,1024]{1,0:T(8,128)S(1)}, s32[1,128]{1,0:T(1,128)S(1)}) custom-call(s32[1]{0:T(128)S(6)} %copy.7.k_ref, s32[3,16,512]{2,1,0:T(8,128)S(1)} %get-tuple-element.12.late, f8e4m3fn[512,1024]{1,0:T(32,128)(4,1)S(1)} %get-tuple-element.13.hm, f8e4m3fn[512,512]{1,0:T(32,128)(4,1)S(1)} %get-tuple-element.14.w1, ...), custom_call_target="tpu_custom_call" | custom-call | tf_op jit(solution)/shard_map/pallas_call | solution.py:362
  36.7 1.5 %shard_map.70 = (f32[512,1024]{1,0:T(8,128)}, s32[3]{0:T(128)}) custom-call(f32[512,1024]{1,0:T(8,128)S(1)} %get-tuple-element.20.support_ref, s32[1,128]{1,0:T(1,128)S(1)} %get-tuple-element.21.cnt_ref), custom_call_target="tpu_custom_call" | custom-call | tf_op jit(solution)/shard_map/pallas_call | solution.py:377
